TPU v7x, 128 devices: a whole 4x4x4 slice. The times are simulated.
128 devices in a mesh: row: 8 (over z, core), col: 16 (over y, x).
Axes of the slice: x: 4, y: 4, z: 4, core: 2. Of those that a mesh axis runs over, the one named last changes fastest.
Arguments:
- features: bfloat16 [64, 524288], P(None, ('row', 'col')), may hold values from -6 to 6
- tile_rows: int32 [8, 16, 512], P('row', 'col'), may hold values from 0 to 511, as said below
- tile_cols: int32 [8, 16, 512], P('row', 'col'), may hold values from 0 to 255
- tile_count: int32 [8, 16], P('row', 'col'), may hold values from 1 to 512, as said below
- tile_data: bfloat16 [8, 16, 512, 128, 128], P('row', 'col'), may hold values from -0.21875 to 0.21875
Outputs:
- filtered: bfloat16 [512, 524288], P(None, ('row', 'col'))
Inputs may be any that keep to these rules, and one draw needn't show every extreme that they name: Within one device the pairs (tile_rows, tile_cols) of all 512 slots are distinct. `tile_count`: some device has all 512 slots live in every draw.
All inputs are finite; a program needn't handle non-finite values.
Results may differ from a plain program's by a relative error of at most 0.009.
Values may be sent and summed in bfloat16 or wider, within the bound.
A program may use at most 128 MiB of HBM per device.

v0:
```python
import jax
import jax.numpy as jnp
from jax import lax
from jax.sharding import PartitionSpec as P

SCALES = 8
TILE_SIZE = 128


def bessel_pair(times):
    halved = times / 2.0
    square = halved * halved
    term_zero = jnp.ones_like(times)
    term_one = halved
    sum_zero = term_zero
    sum_one = term_one
    for degree in range(1, 24):
        term_zero = term_zero * square / float(degree * degree)
        term_one = term_one * square / float(degree * (degree + 1))
        sum_zero = sum_zero + term_zero
        sum_one = sum_one + term_one
    damping = jnp.exp(-times)
    return (damping * sum_zero, damping * sum_one)


def coefficients():
    times = 0.25 * 2.0 ** (jnp.arange(SCALES).astype(jnp.float32) / 2.0)
    bessel_zero, bessel_one = bessel_pair(times)
    return (bessel_zero, -2.0 * bessel_one, 2.0 * (bessel_zero - 2.0 * bessel_one / times))


def tile_products(panel, slot_rows, slot_cols, slot_data, live_count, block_rows):
    channel_count = panel.shape[0]
    blocks = panel.reshape(channel_count, -1, TILE_SIZE)
    slot_total = slot_rows.shape[0]
    group = min(128, slot_total)

    def one_group(step_index, summed):
        start = step_index * group
        row_ids = lax.dynamic_slice_in_dim(slot_rows, start, group, 0)
        col_ids = lax.dynamic_slice_in_dim(slot_cols, start, group, 0)
        entries = lax.dynamic_slice_in_dim(slot_data, start, group, 0)
        picked = jnp.take(blocks, col_ids, axis=1)
        product = jnp.einsum("fgk,grk->fgr", picked, entries, preferred_element_type=jnp.float32)
        live = (start + jnp.arange(group) < live_count).astype(jnp.float32)
        return summed.at[:, row_ids].add(product * live[None, :, None])

    start_sum = jnp.zeros((channel_count, block_rows, TILE_SIZE), jnp.float32)
    group_count = slot_total // group
    summed = lax.fori_loop(0, group_count, one_group, start_sum)
    return summed.reshape(channel_count, block_rows * TILE_SIZE)


def shards(features, tile_rows, tile_cols, tile_count, tile_data):
    col_size = lax.axis_size("col")
    node_count = features.shape[1]
    block_rows = node_count * col_size // TILE_SIZE
    slot_rows = tile_rows.reshape(-1)
    slot_cols = tile_cols.reshape(-1)
    slot_data = tile_data.reshape(-1, TILE_SIZE, TILE_SIZE)
    live_count = tile_count.reshape(())

    def apply_operator(field):
        panel = lax.all_gather(field, "row", axis=1, tiled=True)
        partial_value = tile_products(
            panel, slot_rows, slot_cols, slot_data, live_count, block_rows
        ).astype(jnp.bfloat16)
        owned = lax.psum_scatter(partial_value, "col", scatter_dimension=1, tiled=True).astype(
            jnp.float32
        )
        return owned.astype(jnp.bfloat16)

    first = apply_operator(features)
    second = apply_operator(first)
    coef_zero, coef_one, coef_two = coefficients()
    base = features.astype(jnp.float32)
    first_wide = first.astype(jnp.float32)
    second_wide = second.astype(jnp.float32)
    filtered = (
        coef_zero[:, None, None] * base[None]
        + coef_one[:, None, None] * first_wide[None]
        + coef_two[:, None, None] * (2.0 * second_wide - base)[None]
    )
    return filtered.reshape(-1, node_count).astype(jnp.bfloat16)


def solution(mesh):
    return jax.shard_map(
        shards,
        mesh=mesh,
        in_specs=(
            P(None, ("row", "col")),
            P("row", "col", None),
            P("row", "col", None),
            P("row", "col"),
            P("row", "col", None, None, None),
        ),
        out_specs=P(None, ("row", "col")),
        check_vma=False,
    )
```

profile of v0, /device:TPU:0, one launch (start us, length us, event | category | flops | bytes accessed | tf_op | source)
XLA Modules:
  0.0 556.3 jit_solution(11177541543143327451)
XLA Ops:
  6.5 0.7 all-gather.3.cloned.1.call-update
  7.3 36.5 %all-gather.3.cloned.1.call-done = bf16[64,32768]{1,0:T(8,128)(2,1)} async-done(((bf16[64,4096]{1,0:T(8,128)(2,1)}), bf16[64,32768]{1,0:T(8,128)(2,1)}) %all-gather.3.cloned.1.call-update) | async-done | bytes 4194320 | tf_op jit(solution)/shard_map/all_gather | solution.py:64
  43.8 5.4 copy_bitcast_fusion.3
  49.2 7.9 %broadcast.686.clone = f32[64,512,128]{2,0,1:T(8,128)} broadcast(f32[]{:T(128)} %constant.219.clone.1), dimensions={} | broadcast | bytes 16777220 | tf_op jit(solution)/shard_map/broadcast.105
  57.1 125.7 %while.26 = (s32[]{:T(128)}, f32[64,512,128]{2,0,1:T(8,128)}, s32[512]{0:T(512)S(1)}, bf16[512,128,128]{2,1,0:T(8,128)(2,1)}, s32[512]{0:T(512)S(1)}, /*index=5*...) while((s32[]{:T(128)}, f32[64,512,128]{2,0,1:T(8,128)}, ...), condition=%wide.region_2.0_spmd, body=%wide.region_0.3_spmd.sunk | while | flops 271583744 | bytes 27272112 | solution.py:50
  57.1 0.7 compare_and_fusion.4
  57.9 3.1 gather_fusion
  61.0 7.1 %multiply_bitcast_fusion.4 = f32[128,64,128]{2,1,0:T(8,128)} fusion(bf16[512,128,128]{2,1,0:T(8,128)(2,1)} %get-tuple-element.434, s32[]{:T(128)S(6)} %select_n.69, bf16[128,64,128]{2,1,0:T(8,128)(2,1)S(1)} %gather_fusion, f32[128]{0:T(128)S(1)} %get-tuple-element.397, pred[128]{0:T(512)(128)(4,1)S(1)} %get-tuple-element.398), kind=kOutput, calls=%fused_computation.4.clone.1 | convolution fusion | flops 270532608 | bytes 10486404 | tf_op jit(solution)/shard_map/while/body/eval_jaxpr/fgk,grk->fgr/dot_general | solution.py:44
  68.1 0.1 compare_select_fusion.8
  68.1 20.4 %scatter_fusion = f32[64,512,128]{2,0,1:T(8,128)} fusion(f32[64,512,128]{2,0,1:T(8,128)} %get-tuple-element.421, s32[128]{0:T(128)S(1)} %compare_select_fusion.8, f32[128,64,128]{2,1,0:T(8,128)} %multiply_bitcast_fusion.4), kind=kCustom, calls=%fused_computation.2.clone.1 | custom fusion | flops 1048576 | bytes 12583424 | tf_op jit(solution)/shard_map/while/body/eval_jaxpr/scatter-add | solution.py:46
  88.6 0.7 compare_and_fusion.4
  89.3 3.1 gather_fusion
  92.5 7.1 %multiply_bitcast_fusion.4 = f32[128,64,128]{2,1,0:T(8,128)} fusion(bf16[512,128,128]{2,1,0:T(8,128)(2,1)} %get-tuple-element.434, s32[]{:T(128)S(6)} %select_n.69, bf16[128,64,128]{2,1,0:T(8,128)(2,1)S(1)} %gather_fusion, f32[128]{0:T(128)S(1)} %get-tuple-element.397, pred[128]{0:T(512)(128)(4,1)S(1)} %get-tuple-element.398), kind=kOutput, calls=%fused_computation.4.clone.1 | convolution fusion | flops 270532608 | bytes 10486404 | tf_op jit(solution)/shard_map/while/body/eval_jaxpr/fgk,grk->fgr/dot_general | solution.py:44
  99.5 0.1 compare_select_fusion.8
  99.6 20.4 %scatter_fusion = f32[64,512,128]{2,0,1:T(8,128)} fusion(f32[64,512,128]{2,0,1:T(8,128)} %get-tuple-element.421, s32[128]{0:T(128)S(1)} %compare_select_fusion.8, f32[128,64,128]{2,1,0:T(8,128)} %multiply_bitcast_fusion.4), kind=kCustom, calls=%fused_computation.2.clone.1 | custom fusion | flops 1048576 | bytes 12583424 | tf_op jit(solution)/shard_map/while/body/eval_jaxpr/scatter-add | solution.py:46
  120.0 0.7 compare_and_fusion.4
  120.7 3.1 gather_fusion
  123.9 7.1 %multiply_bitcast_fusion.4 = f32[128,64,128]{2,1,0:T(8,128)} fusion(bf16[512,128,128]{2,1,0:T(8,128)(2,1)} %get-tuple-element.434, s32[]{:T(128)S(6)} %select_n.69, bf16[128,64,128]{2,1,0:T(8,128)(2,1)S(1)} %gather_fusion, f32[128]{0:T(128)S(1)} %get-tuple-element.397, pred[128]{0:T(512)(128)(4,1)S(1)} %get-tuple-element.398), kind=kOutput, calls=%fused_computation.4.clone.1 | convolution fusion | flops 270532608 | bytes 10486404 | tf_op jit(solution)/shard_map/while/body/eval_jaxpr/fgk,grk->fgr/dot_general | solution.py:44
  130.9 0.1 compare_select_fusion.8
  131.0 20.4 %scatter_fusion = f32[64,512,128]{2,0,1:T(8,128)} fusion(f32[64,512,128]{2,0,1:T(8,128)} %get-tuple-element.421, s32[128]{0:T(128)S(1)} %compare_select_fusion.8, f32[128,64,128]{2,1,0:T(8,128)} %multiply_bitcast_fusion.4), kind=kCustom, calls=%fused_computation.2.clone.1 | custom fusion | flops 1048576 | bytes 12583424 | tf_op jit(solution)/shard_map/while/body/eval_jaxpr/scatter-add | solution.py:46
  151.4 0.7 compare_and_fusion.4
  152.1 3.1 gather_fusion
  155.3 7.1 %multiply_bitcast_fusion.4 = f32[128,64,128]{2,1,0:T(8,128)} fusion(bf16[512,128,128]{2,1,0:T(8,128)(2,1)} %get-tuple-element.434, s32[]{:T(128)S(6)} %select_n.69, bf16[128,64,128]{2,1,0:T(8,128)(2,1)S(1)} %gather_fusion, f32[128]{0:T(128)S(1)} %get-tuple-element.397, pred[128]{0:T(512)(128)(4,1)S(1)} %get-tuple-element.398), kind=kOutput, calls=%fused_computation.4.clone.1 | convolution fusion | flops 270532608 | bytes 10486404 | tf_op jit(solution)/shard_map/while/body/eval_jaxpr/fgk,grk->fgr/dot_general | solution.py:44
  162.4 0.1 compare_select_fusion.8
  162.4 20.4 %scatter_fusion = f32[64,512,128]{2,0,1:T(8,128)} fusion(f32[64,512,128]{2,0,1:T(8,128)} %get-tuple-element.421, s32[128]{0:T(128)S(1)} %compare_select_fusion.8, f32[128,64,128]{2,1,0:T(8,128)} %multiply_bitcast_fusion.4), kind=kCustom, calls=%fused_computation.2.clone.1 | custom fusion | flops 1048576 | bytes 12583424 | tf_op jit(solution)/shard_map/while/body/eval_jaxpr/scatter-add | solution.py:46
  182.8 9.0 %copy_bitcast_fusion.1 = bf16[64,65536]{1,0:T(8,128)(2,1)} fusion(f32[64,512,128]{2,0,1:T(8,128)} %get-tuple-element.254), kind=kLoop, calls=%fused_computation.33 | loop fusion | flops 4194304 | bytes 25165824 | tf_op jit(solution)/shard_map/convert_element_type | solution.py:67
  191.9 85.7 %reduce-scatter.3.cloned.1.call-done = bf16[64,4096]{1,0:T(8,128)(2,1)} async-done(((bf16[64,65536]{1,0:T(8,128)(2,1)}), bf16[64,4096]{1,0:T(8,128)(2,1)}) %reduce-scatter.3.cloned.1.call-update) | async-done | bytes 524304 | tf_op jit(solution)/shard_map/reduce_scatter | solution.py:68
  277.6 0.2 reduce-scatter.5.cloned.1.call-start
  277.8 33.2 %all-gather.5.cloned.1.call-done = bf16[64,32768]{1,0:T(8,128)(2,1)} async-done(((bf16[64,4096]{1,0:T(8,128)(2,1)}), bf16[64,32768]{1,0:T(8,128)(2,1)}) %all-gather.5.cloned.1.call-update) | async-done | bytes 4194320 | tf_op jit(solution)/shard_map/all_gather | solution.py:64
  311.0 5.4 copy_bitcast_fusion.2
  316.4 7.9 %broadcast.686 = f32[64,512,128]{2,0,1:T(8,128)} broadcast(f32[]{:T(128)} %constant.219.clone.1), dimensions={} | broadcast | bytes 16777220 | tf_op jit(solution)/shard_map/broadcast.105
  324.3 125.7 %while.27 = (s32[]{:T(128)}, f32[64,512,128]{2,0,1:T(8,128)}, s32[512]{0:T(512)S(1)}, bf16[512,128,128]{2,1,0:T(8,128)(2,1)}, s32[512]{0:T(512)S(1)}, /*index=5*...) while((s32[]{:T(128)}, f32[64,512,128]{2,0,1:T(8,128)}, ...), condition=%wide.region_6.0_spmd, body=%wide.region_4.0_spmd.sunk | while | flops 271583744 | bytes 27272112 | solution.py:50
  324.3 0.7 compare_and_fusion.5
  325.0 3.1 gather_fusion.1
  328.2 7.1 %multiply_bitcast_fusion.5 = f32[128,64,128]{2,1,0:T(8,128)} fusion(bf16[512,128,128]{2,1,0:T(8,128)(2,1)} %get-tuple-element.467, s32[]{:T(128)S(6)} %select_n.72, bf16[128,64,128]{2,1,0:T(8,128)(2,1)S(1)} %gather_fusion.1, f32[128]{0:T(128)S(1)} %get-tuple-element.407, pred[128]{0:T(512)(128)(4,1)S(1)} %get-tuple-element.408), kind=kOutput, calls=%fused_computation.18.clone.1 | convolution fusion | flops 270532608 | bytes 10486404 | tf_op jit(solution)/shard_map/while/body/eval_jaxpr/fgk,grk->fgr/dot_general | solution.py:44
  335.2 0.1 compare_select_fusion.9
  335.3 20.4 %scatter_fusion.1 = f32[64,512,128]{2,0,1:T(8,128)} fusion(f32[64,512,128]{2,0,1:T(8,128)} %get-tuple-element.454, s32[128]{0:T(128)S(1)} %compare_select_fusion.9, f32[128,64,128]{2,1,0:T(8,128)} %multiply_bitcast_fusion.5), kind=kCustom, calls=%fused_computation.3.clone.1 | custom fusion | flops 1048576 | bytes 12583424 | tf_op jit(solution)/shard_map/while/body/eval_jaxpr/scatter-add | solution.py:46
  355.7 0.7 compare_and_fusion.5
  356.5 3.1 gather_fusion.1
  359.6 7.1 %multiply_bitcast_fusion.5 = f32[128,64,128]{2,1,0:T(8,128)} fusion(bf16[512,128,128]{2,1,0:T(8,128)(2,1)} %get-tuple-element.467, s32[]{:T(128)S(6)} %select_n.72, bf16[128,64,128]{2,1,0:T(8,128)(2,1)S(1)} %gather_fusion.1, f32[128]{0:T(128)S(1)} %get-tuple-element.407, pred[128]{0:T(512)(128)(4,1)S(1)} %get-tuple-element.408), kind=kOutput, calls=%fused_computation.18.clone.1 | convolution fusion | flops 270532608 | bytes 10486404 | tf_op jit(solution)/shard_map/while/body/eval_jaxpr/fgk,grk->fgr/dot_general | solution.py:44
  366.7 0.1 compare_select_fusion.9
  366.8 20.4 %scatter_fusion.1 = f32[64,512,128]{2,0,1:T(8,128)} fusion(f32[64,512,128]{2,0,1:T(8,128)} %get-tuple-element.454, s32[128]{0:T(128)S(1)} %compare_select_fusion.9, f32[128,64,128]{2,1,0:T(8,128)} %multiply_bitcast_fusion.5), kind=kCustom, calls=%fused_computation.3.clone.1 | custom fusion | flops 1048576 | bytes 12583424 | tf_op jit(solution)/shard_map/while/body/eval_jaxpr/scatter-add | solution.py:46
  387.1 0.7 compare_and_fusion.5
  387.9 3.1 gather_fusion.1
  391.0 7.1 %multiply_bitcast_fusion.5 = f32[128,64,128]{2,1,0:T(8,128)} fusion(bf16[512,128,128]{2,1,0:T(8,128)(2,1)} %get-tuple-element.467, s32[]{:T(128)S(6)} %select_n.72, bf16[128,64,128]{2,1,0:T(8,128)(2,1)S(1)} %gather_fusion.1, f32[128]{0:T(128)S(1)} %get-tuple-element.407, pred[128]{0:T(512)(128)(4,1)S(1)} %get-tuple-element.408), kind=kOutput, calls=%fused_computation.18.clone.1 | convolution fusion | flops 270532608 | bytes 10486404 | tf_op jit(solution)/shard_map/while/body/eval_jaxpr/fgk,grk->fgr/dot_general | solution.py:44
  398.1 0.1 compare_select_fusion.9
  398.2 20.4 %scatter_fusion.1 = f32[64,512,128]{2,0,1:T(8,128)} fusion(f32[64,512,128]{2,0,1:T(8,128)} %get-tuple-element.454, s32[128]{0:T(128)S(1)} %compare_select_fusion.9, f32[128,64,128]{2,1,0:T(8,128)} %multiply_bitcast_fusion.5), kind=kCustom, calls=%fused_computation.3.clone.1 | custom fusion | flops 1048576 | bytes 12583424 | tf_op jit(solution)/shard_map/while/body/eval_jaxpr/scatter-add | solution.py:46
  418.6 0.7 compare_and_fusion.5
  419.3 3.1 gather_fusion.1
  422.5 7.1 %multiply_bitcast_fusion.5 = f32[128,64,128]{2,1,0:T(8,128)} fusion(bf16[512,128,128]{2,1,0:T(8,128)(2,1)} %get-tuple-element.467, s32[]{:T(128)S(6)} %select_n.72, bf16[128,64,128]{2,1,0:T(8,128)(2,1)S(1)} %gather_fusion.1, f32[128]{0:T(128)S(1)} %get-tuple-element.407, pred[128]{0:T(512)(128)(4,1)S(1)} %get-tuple-element.408), kind=kOutput, calls=%fused_computation.18.clone.1 | convolution fusion | flops 270532608 | bytes 10486404 | tf_op jit(solution)/shard_map/while/body/eval_jaxpr/fgk,grk->fgr/dot_general | solution.py:44
  429.5 0.1 compare_select_fusion.9
  429.6 20.4 %scatter_fusion.1 = f32[64,512,128]{2,0,1:T(8,128)} fusion(f32[64,512,128]{2,0,1:T(8,128)} %get-tuple-element.454, s32[128]{0:T(128)S(1)} %compare_select_fusion.9, f32[128,64,128]{2,1,0:T(8,128)} %multiply_bitcast_fusion.5), kind=kCustom, calls=%fused_computation.3.clone.1 | custom fusion | flops 1048576 | bytes 12583424 | tf_op jit(solution)/shard_map/while/body/eval_jaxpr/scatter-add | solution.py:46
  450.0 9.0 %copy_bitcast_fusion = bf16[64,65536]{1,0:T(8,128)(2,1)} fusion(f32[64,512,128]{2,0,1:T(8,128)} %get-tuple-element.255), kind=kLoop, calls=%fused_computation.32 | loop fusion | flops 4194304 | bytes 25165824 | tf_op jit(solution)/shard_map/convert_element_type | solution.py:67
  459.0 1.0 copy-done
  460.1 0.1 mul.774
  460.2 0.1 mul.775
  460.4 0.1 mul.805
  460.4 0.1 mul.806
  460.6 0.1 mul.813
  460.6 0.1 mul.814
  460.7 0.1 convert_element_type.71
  460.8 83.8 %reduce-scatter.5.cloned.1.call-done = bf16[64,4096]{1,0:T(8,128)(2,1)} async-done(((bf16[64,65536]{1,0:T(8,128)(2,1)}), bf16[64,4096]{1,0:T(8,128)(2,1)}) %reduce-scatter.5.cloned.1.call-update) | async-done | bytes 524304 | tf_op jit(solution)/shard_map/reduce_scatter | solution.py:68
  544.6 1.2 multiply_subtract_fusion
  545.8 3.9 fusion.21
  (25 shorter events, 0.4 us)
Async XLA Ops:
  6.5 37.3 %all-gather.3.cloned.1.call-start = ((), (), s32[]{:S(2)}) async-start(), calls=%async_computation.2 | async-start | bytes 4718592 | tf_op jit(solution)/shard_map/all_gather | solution.py:64
  7.3 270.3 %reduce-scatter.3.cloned.1.call-start = ((), (), s32[]{:S(2)}) async-start(), calls=%async_computation.3 | async-start | bytes 8912896 | tf_op jit(solution)/shard_map/reduce_scatter | solution.py:68
  49.2 7.9 %copy-start.2 = (s32[1,1,512]{2,1,0:T(1,128)S(1)}, s32[1,1,512]{2,1,0:T(1,128)}, u32[]{:S(2)}) copy-start(s32[1,1,512]{2,1,0:T(1,128)} %param.13) | copy-start | bytes 6148
  49.2 7.9 %copy-start.3 = (s32[1,1,512]{2,1,0:T(1,128)S(1)}, s32[1,1,512]{2,1,0:T(1,128)}, u32[]{:S(2)}) copy-start(s32[1,1,512]{2,1,0:T(1,128)} %param.12) | copy-start | bytes 6148
  191.8 119.2 %all-gather.5.cloned.1.call-start = ((), (), s32[]{:S(2)}) async-start(), calls=%async_computation.4 | async-start | bytes 4718592 | tf_op jit(solution)/shard_map/all_gather | solution.py:64
  277.6 267.0 %reduce-scatter.5.cloned.1.call-start = ((), (), s32[]{:S(2)}) async-start(), calls=%async_computation.5 | async-start | bytes 8912896 | tf_op jit(solution)/shard_map/reduce_scatter | solution.py:68
  459.0 1.0 copy-start
  459.0 1.8 copy-start.1
Sparse Core Ops, SparseCore 0:
  9.0 34.7 all-gather.2
  192.0 85.5 reduce-scatter.2
  279.3 31.6 all-gather.4
  459.1 85.4 reduce-scatter.4
where the time goes:
time: 559 us; the launch traced here: 556 us
  waiting for transfers between devices  240 us (43%)
  other arithmetic  193 us (35%)
  matrix products  56.5 us (10%)
  local copies, waits for them, and re-layouts  53.2 us (10%)
  between operations  13.2 us (2%)
    reduce_scatter x2, waiting for transfers between devices, apply_operator(): lax.psum_scatter(partial_value, 'col', scatter_dimension=1, tiled=True)  169 us
    scatter-add x8, other arithmetic, one_group(): return summed.at[:, row_ids].add(product * live[None, :, None])  163 us
    all_gather x2, waiting for transfers between devices, apply_operator(): panel = lax.all_gather(field, 'row', axis=1, tiled=True)  69.7 us
    dot_general x8, matrix products, one_group(): jnp.einsum('fgk,grk->fgr', picked, entries, preferred_element_type=jnp.fl...  56.5 us
    gather x8, local copies, waits for them, and re-layouts, one_group(): picked = jnp.take(blocks, col_ids, axis=1)  25.1 us
    convert_element_type x2, other arithmetic, apply_operator(): partial_value = tile_products(panel, slot_rows, slot_cols, slot_data, liv...  18 us
    another operation x2, local copies, waits for them, and re-layouts  15.8 us
  transfers between devices with their start and end apart: 4, of which 4 were waited for; matrix products, arithmetic and copies ran while one was open for 0% of the time, Pallas kernels for 0%

commit v1 on v0

v1 whole, which is shorter than its diff:
```python
import functools

import jax
import jax.numpy as jnp
from jax import lax
from jax.experimental import pallas as pl
from jax.experimental.pallas import tpu as pltpu
from jax.sharding import PartitionSpec as P

TILE = 128
SLOTS = 512
CHANNELS = 64
CHUNKS = 2
CH = CHANNELS // CHUNKS
SCALES = 8
OWN = 32
UNROLL = 16
MESH = pl.DeviceIdType.MESH
BF = jnp.bfloat16
F32 = jnp.float32


def bessel_pair(times):
    halved = times / 2.0
    square = halved * halved
    term_zero = jnp.ones_like(times)
    term_one = halved
    sum_zero = term_zero
    sum_one = term_one
    for degree in range(1, 24):
        term_zero = term_zero * square / float(degree * degree)
        term_one = term_one * square / float(degree * (degree + 1))
        sum_zero = sum_zero + term_zero
        sum_one = sum_one + term_one
    damping = jnp.exp(-times)
    return (damping * sum_zero, damping * sum_one)


def coefficients():
    times = 0.25 * 2.0 ** (jnp.arange(SCALES).astype(jnp.float32) / 2.0)
    bessel_zero, bessel_one = bessel_pair(times)
    return (bessel_zero, -2.0 * bessel_one, 2.0 * (bessel_zero - 2.0 * bessel_one / times))


def slot_tables(slot_rows, slot_cols, live_count):
    ids = jnp.arange(SLOTS, dtype=jnp.int32)
    row = jnp.where(ids < live_count, slot_rows, SLOTS)
    key = row * SLOTS + ids
    rank = jnp.sum((key[None, :] < key[:, None]).astype(jnp.int32), axis=1)
    hit = rank[:, None] == ids[None, :]
    packed = (row * SLOTS + ids) * 256 + slot_cols
    ordered = jnp.sum(jnp.where(hit, packed[:, None], 0), axis=0)
    cols = ordered % 256
    perm = (ordered // 256) % SLOTS
    rows = ordered // (256 * SLOTS)
    before = jnp.concatenate([jnp.full((1,), -1, jnp.int32), rows[:-1]])
    keep = (rows == before).astype(F32)
    upto = jnp.sum((row[:, None] <= ids[None, :]).astype(jnp.int32), axis=0)
    here = jnp.sum((row[:, None] == ids[None, :]).astype(jnp.int32), axis=0)
    last = jnp.where(here > 0, upto - 1, SLOTS)
    return perm, cols, keep, last


def chain_kernel(
    perm, cols, keep, last, feat, tdata, first_out, second_out,
    tiles, f00, f01, f10, f11, runs, p0, p1,
    r00, r01, r10, r11, q00, q01, q10, q11,
    tile_sem, s1, v1, s2, v2, sa, va,
):
    row = lax.axis_index("row")
    col = lax.axis_index("col")
    z, core = row // 2, row % 2
    y, x = col // 4, col % 4
    fields = ((f00, f01), (f10, f11))
    parts = (p0, p1)
    recv1 = ((r00, r01), (r10, r11))
    recv2 = ((q00, q01), (q10, q11))
    outs = (first_out, second_out)

    def up(v):
        return (v + 1) % 4

    def down(v):
        return (v + 3) % 4

    def far(v):
        return (v + 2) % 4

    z_next = (up(z) * 2 + core, col)
    z_prev = (down(z) * 2 + core, col)
    mate = (z * 2 + (1 - core), col)
    x_next = (row, y * 4 + up(x))
    x_prev = (row, y * 4 + down(x))
    y_next = (row, up(y) * 4 + x)
    y_prev = (row, down(y) * 4 + x)

    barrier = pltpu.get_barrier_semaphore()
    for other in (z_next, z_prev, mate, x_next, x_prev, y_next, y_prev):
        pl.semaphore_signal(barrier, inc=1, device_id=other, device_id_type=MESH)

    tile_copy = pltpu.make_async_copy(tdata, tiles, tile_sem)
    tile_copy.start()

    def send(src, dst, ssem, rsem, to):
        return pltpu.make_async_remote_copy(
            src_ref=src, dst_ref=dst, send_sem=ssem, recv_sem=rsem,
            device_id=to, device_id_type=MESH,
        )

    def gather(a, k):
        ref = fields[a][k]
        half = OWN // 2

        def block(zz, h=None):
            start = (zz * 2 + core) * OWN
            if h is None:
                return ref.at[pl.ds(start, OWN)]
            return ref.at[pl.ds(start + h * half, half)]

        def copy(i, view, to):
            return send(view, view, sa.at[a, k, i], va.at[a, k, i], to)

        zp, zn, zf = down(z), up(z), far(z)
        return [
            copy(0, block(z, 0), z_next),
            copy(1, block(z, 1), z_next),
            copy(2, block(z, 0), z_prev),
            copy(3, block(z, 1), z_prev),
            copy(4, block(zp, 0), z_next),
            copy(5, block(zn, 1), z_prev),
            copy(6, block(z), mate),
            copy(7, block(zp, 0), mate),
            copy(8, block(zp, 1), mate),
            copy(9, block(zn, 0), mate),
            copy(10, block(zn, 1), mate),
            copy(11, block(zf, 0), mate),
            copy(12, block(zf, 1), mate),
        ]

    def gather_start(g):
        g[0].start()
        g[3].start()
        g[1].start()
        g[2].start()
        g[6].start()

    def gather_relay(g):
        g[0].wait_recv()
        g[4].start()
        g[7].start()
        g[3].wait_recv()
        g[5].start()
        g[10].start()

    def gather_finish(g):
        g[1].wait_recv()
        g[8].start()
        g[2].wait_recv()
        g[9].start()
        g[4].wait_recv()
        g[11].start()
        g[5].wait_recv()
        g[12].start()
        for i in range(6, 13):
            g[i].wait_recv()

    def gather_sent(g):
        for c in g:
            c.wait_send()

    def products(a, k, begin, end, acc):
        field = fields[a][k]

        def trip(i, acc):
            for u in range(UNROLL):
                s = i * UNROLL + u
                product = lax.dot_general(
                    field[cols[s]], tiles[perm[s]], (((1,), (1,)), ((), ())),
                    preferred_element_type=F32,
                )
                acc = acc * keep[s] + product
                runs[s] = acc.astype(BF)
            return acc

        return lax.fori_loop(begin // UNROLL, end // UNROLL, trip, acc)

    def zero():
        return jnp.zeros((CH, TILE), F32)

    def pack(k):
        part = parts[k]

        def trip(i, carry):
            for xx in range(4):
                for u in range(8):
                    b = (i // 4) * 128 + xx * 32 + (i % 4) * 8 + u
                    part[i // 4, xx, (i % 4) * 8 + u] = runs[last[b]]
            return carry

        lax.fori_loop(0, 16, trip, 0)

    def scatter1(a, k):
        part, got = parts[k], recv1[a][k]
        out = []
        for st in range(2):
            base = st * 16
            me = x if st == 0 else y
            nxt = x_next if st == 0 else y_next
            prv = x_prev if st == 0 else y_prev

            def view(who, h, st=st, base=base):
                if st == 0:
                    return part.at[:, who, pl.ds(base + 8 * h, 8)]
                return part.at[who, :, pl.ds(base + 8 * h, 8)]

            rows = []
            for d in range(2):
                to = nxt if d == 0 else prv
                near = up(me) if d == 0 else down(me)
                views = (view(far(me), d), view(near, 1 - d), view(near, d))
                rows.append([
                    send(views[m], got.at[st, d, m], s1.at[a, k, st, d, m], v1.at[a, k, st, d, m], to)
                    for m in range(3)
                ])
            out.append(rows)
        return out

    def scatter2(a, k):
        part, got = parts[k], recv2[a][k]
        out = []
        for st in range(2):
            base = st * 16
            me = y if st == 0 else x
            nxt = y_next if st == 0 else x_next
            prv = y_prev if st == 0 else x_prev

            def view(who, h, st=st, base=base):
                if st == 0:
                    return part.at[who, x, pl.ds(base + 8 * h, 8)]
                return part.at[y, who, pl.ds(base + 8 * h, 8)]

            rows = []
            for d in range(2):
                to = nxt if d == 0 else prv
                near = up(me) if d == 0 else down(me)
                views = (view(far(me), d), view(near, 1 - d), view(near, d))
                rows.append([
                    send(views[m], got.at[st, d, m], s2.at[a, k, st, d, m], v2.at[a, k, st, d, m], to)
                    for m in range(3)
                ])
            out.append(rows)
        return out

    def start_messages(copies, m):
        for st in range(2):
            for d in range(2):
                copies[st][d][m].start()

    def carry1(a, k, copies):
        part, got = parts[k], recv1[a][k]
        for st in range(2):
            me = x if st == 0 else y
            for d in range(2):
                near = up(me) if d == 0 else down(me)
                lo = st * 16 + 8 * d
                copies[st][d][0].wait_recv()

                def trip(i, c, st=st, d=d, near=near, lo=lo):
                    for u in range(8):
                        there = got[st, d, 0, i, u].astype(F32)
                        if st == 0:
                            mine = part[i, near, lo + u].astype(F32)
                            part[i, near, lo + u] = (mine + there).astype(BF)
                        else:
                            mine = part[near, i, lo + u].astype(F32)
                            part[near, i, lo + u] = (mine + there).astype(BF)
                    return c

                lax.fori_loop(0, 4, trip, 0)
                copies[st][d][2].start()

    def close1(a, k, copies):
        part, got = parts[k], recv1[a][k]
        for m in (1, 2):
            for st in range(2):
                for d in range(2):
                    copies[st][d][m].wait_recv()
        for st in range(2):
            for h in range(2):
                lo = st * 16 + 8 * h

                def trip(i, c, st=st, h=h, lo=lo):
                    for u in range(8):
                        total = (
                            got[st, h, 2, i, u].astype(F32) + got[st, 1 - h, 1, i, u].astype(F32)
                        )
                        if st == 0:
                            part[i, x, lo + u] = (part[i, x, lo + u].astype(F32) + total).astype(BF)
                        else:
                            part[y, i, lo + u] = (part[y, i, lo + u].astype(F32) + total).astype(BF)
                    return c

                lax.fori_loop(0, 4, trip, 0)

    def carry2(a, k, copies):
        part, got = parts[k], recv2[a][k]
        for st in range(2):
            me = y if st == 0 else x
            for d in range(2):
                near = up(me) if d == 0 else down(me)
                lo = st * 16 + 8 * d
                copies[st][d][0].wait_recv()
                for u in range(8):
                    there = got[st, d, 0, u].astype(F32)
                    if st == 0:
                        part[near, x, lo + u] = (part[near, x, lo + u].astype(F32) + there).astype(BF)
                    else:
                        part[y, near, lo + u] = (part[y, near, lo + u].astype(F32) + there).astype(BF)
                copies[st][d][2].start()

    def close2(a, k, copies):
        part, got = parts[k], recv2[a][k]
        for m in (1, 2):
            for st in range(2):
                for d in range(2):
                    copies[st][d][m].wait_recv()
        for st in range(2):
            for h in range(2):
                for u in range(8):
                    b = st * 16 + 8 * h + u
                    total = (
                        part[y, x, b].astype(F32)
                        + got[st, h, 2, u].astype(F32)
                        + got[st, 1 - h, 1, u].astype(F32)
                    ).astype(BF)
                    outs[a][k, b] = total
                    if a == 0:
                        fields[1][k][row * OWN + b] = total

    def scatter_sent(*many):
        for copies in many:
            for st in range(2):
                for d in range(2):
                    for m in range(3):
                        copies[st][d][m].wait_send()

    for k in range(CHUNKS):
        for j in range(OWN):
            fields[0][k][row * OWN + j] = feat[k * CH:(k + 1) * CH, j * TILE:(j + 1) * TILE]
    runs[SLOTS] = jnp.zeros((CH, TILE), BF)

    pl.semaphore_wait(barrier, 7)
    g = [[gather(a, k) for k in range(CHUNKS)] for a in range(2)]
    c1 = [[scatter1(a, k) for k in range(CHUNKS)] for a in range(2)]
    c2 = [[scatter2(a, k) for k in range(CHUNKS)] for a in range(2)]

    gather_start(g[0][0])
    gather_relay(g[0][0])
    gather_start(g[0][1])
    gather_finish(g[0][0])
    tile_copy.wait()

    for a in range(2):
        acc = products(a, 0, 0, SLOTS // 2, zero())
        gather_relay(g[a][1])
        products(a, 0, SLOTS // 2, SLOTS, acc)
        if a == 1:
            scatter_sent(c1[0][0], c2[0][0])
        pack(0)
        start_messages(c1[a][0], 0)
        start_messages(c1[a][0], 1)
        gather_finish(g[a][1])
        products(a, 1, 0, SLOTS, zero())
        carry1(a, 0, c1[a][0])
        if a == 1:
            scatter_sent(c1[0][1], c2[0][1])
        pack(1)
        start_messages(c1[a][1], 0)
        close1(a, 0, c1[a][0])
        start_messages(c2[a][0], 0)
        start_messages(c2[a][0], 1)
        start_messages(c1[a][1], 1)
        carry2(a, 0, c2[a][0])
        carry1(a, 1, c1[a][1])
        close2(a, 0, c2[a][0])
        if a == 0:
            gather_start(g[1][0])
        close1(a, 1, c1[a][1])
        start_messages(c2[a][1], 0)
        start_messages(c2[a][1], 1)
        if a == 0:
            gather_relay(g[1][0])
        carry2(a, 1, c2[a][1])
        if a == 0:
            gather_finish(g[1][0])
        close2(a, 1, c2[a][1])
        if a == 0:
            gather_start(g[1][1])

    for a in range(2):
        for k in range(CHUNKS):
            gather_sent(g[a][k])
    scatter_sent(c1[1][0], c2[1][0], c1[1][1], c2[1][1])


def combine_kernel(coef, feat, first, second, out):
    for k in range(CHUNKS):
        for j in range(OWN):
            nodes = slice(j * TILE, (j + 1) * TILE)
            base = feat[k * CH:(k + 1) * CH, nodes].astype(F32)
            one = first[k, j].astype(F32)
            two = 2.0 * second[k, j].astype(F32) - base
            for s in range(SCALES):
                value = coef[0, s] * base + coef[1, s] * one + coef[2, s] * two
                out[s * CHANNELS + k * CH:s * CHANNELS + (k + 1) * CH, nodes] = value.astype(BF)


def shards(features, tile_rows, tile_cols, tile_count, tile_data):
    perm, cols, keep, last = slot_tables(
        tile_rows.reshape(-1), tile_cols.reshape(-1), tile_count.reshape(())
    )
    smem = pl.BlockSpec(memory_space=pltpu.SMEM)
    vmem = pl.BlockSpec(memory_space=pltpu.VMEM)
    half = jax.ShapeDtypeStruct((CHUNKS, OWN, CH, TILE), BF)
    field = pltpu.VMEM((8 * OWN, CH, TILE), BF)
    part = pltpu.VMEM((4, 4, OWN, CH, TILE), BF)
    got1 = pltpu.VMEM((2, 2, 3, 4, 8, CH, TILE), BF)
    got2 = pltpu.VMEM((2, 2, 3, 8, CH, TILE), BF)
    dma = pltpu.SemaphoreType.DMA
    first, second = pl.pallas_call(
        chain_kernel,
        out_shape=(half, half),
        in_specs=[smem, smem, smem, smem, vmem, pl.BlockSpec(memory_space=pl.ANY)],
        out_specs=(vmem, vmem),
        scratch_shapes=[
            pltpu.VMEM((SLOTS, TILE, TILE), BF),
            field, field, field, field,
            pltpu.VMEM((SLOTS + 1, CH, TILE), BF),
            part, part,
            got1, got1, got1, got1,
            got2, got2, got2, got2,
            dma,
            dma((2, CHUNKS, 2, 2, 3)), dma((2, CHUNKS, 2, 2, 3)),
            dma((2, CHUNKS, 2, 2, 3)), dma((2, CHUNKS, 2, 2, 3)),
            dma((2, CHUNKS, 13)), dma((2, CHUNKS, 13)),
        ],
        compiler_params=pltpu.CompilerParams(
            collective_id=0, has_side_effects=True, vmem_limit_bytes=62 * 1024 * 1024
        ),
        name="chain",
    )(perm, cols, keep, last, features, tile_data.reshape(SLOTS, TILE, TILE))

    coef = jnp.stack(coefficients())
    return pl.pallas_call(
        combine_kernel,
        out_shape=jax.ShapeDtypeStruct((SCALES * CHANNELS, OWN * TILE), BF),
        in_specs=[smem, vmem, vmem, vmem],
        out_specs=vmem,
        name="combine",
    )(coef, features, first, second)


def solution(mesh):
    return jax.shard_map(
        shards,
        mesh=mesh,
        in_specs=(
            P(None, ("row", "col")),
            P("row", "col", None),
            P("row", "col", None),
            P("row", "col"),
            P("row", "col", None, None, None),
        ),
        out_specs=P(None, ("row", "col")),
        check_vma=False,
    )
```

time: 559 us -> 165 us (0.30)
  waiting for transfers between devices: 240 us -> 0 us
  other arithmetic: 193 us -> 4.77 us
  Pallas kernels: 0 us -> 159 us
  matrix products: 56.5 us -> 0 us
  local copies, waits for them, and re-layouts: 53.2 us -> 0 us
  between operations: 13.2 us -> 0.67 us
    reduce_scatter x2 -> x0, waiting for transfers between devices: 169 us -> none  [apply_operator(): lax.psum_scatter(partial_value, 'col', scatter_dimension=1, tiled=True)]
    scatter-add x8 -> x0, other arithmetic: 163 us -> none  [one_group(): return summed.at[:, row_ids].add(product * live[None, :, None])]
    pallas_call x0 -> x2, Pallas kernels: none -> 159 us  [the longest x1 154 us: shards(): pl.pallas_call(chain_kernel, out_shape=(half, half), in_specs=[smem, smem...]
    all_gather x2 -> x0, waiting for transfers between devices: 69.7 us -> none  [apply_operator(): panel = lax.all_gather(field, 'row', axis=1, tiled=True)]
    dot_general x8 -> x0, matrix products: 56.5 us -> none  [one_group(): jnp.einsum('fgk,grk->fgr', picked, entries, preferred_element_type=jnp.fl...]
    gather x8 -> x0, local copies, waits for them, and re-layouts: 25.1 us -> none  [one_group(): picked = jnp.take(blocks, col_ids, axis=1)]
    convert_element_type x5 -> x1, other arithmetic: 22.1 us -> 0.64 us  [slot_tables(): keep = (rows == before).astype(F32)]
    another operation x2 -> x0, local copies, waits for them, and re-layouts: 15.8 us -> none
  transfers between devices with their start and end apart: 4 -> 0, of which waited for: 4 -> 0; matrix products, arithmetic and copies ran while one was open for 0% -> 0% of each run, Pallas kernels for 0% -> 0%
where the time goes in v1:
time: 165 us; the launch traced here: 164 us
  Pallas kernels  159 us (96%)
  other arithmetic  4.77 us (3%)
    pallas_call x1, Pallas kernels, shards(): pl.pallas_call(chain_kernel, out_shape=(half, half), in_specs=[smem, smem...  154 us
    pallas_call x1, Pallas kernels, shards(): pl.pallas_call(combine_kernel, out_shape=jax.ShapeDtypeStruct((SCALES * C...  5.27 us

profile of v1, /device:TPU:0, one launch (start us, length us, event | category | flops | bytes accessed | tf_op | source)
XLA Modules:
  0.0 164.4 jit_solution(9747950830260312616)
XLA Ops:
  0.7 0.1 broadcast_multiply_fusion
  0.7 0.1 subtract_multiply_fusion
  0.8 0.6 pad_maximum_fusion.coef
  1.4 0.7 iota_add_fusion
  2.1 0.7 multiply_add_fusion
  2.8 0.6 convert_reduce_fusion.1
  3.4 0.2 select_reduce_fusion
  3.6 0.6 add_select_fusion.4.last
  4.2 0.6 add_select_fusion
  4.8 0.6 fusion.3.keep
  5.4 153.7 %chain.1 = (bf16[2,32,32,128]{3,2,1,0:T(8,128)(2,1)}, bf16[2,32,32,128]{3,2,1,0:T(8,128)(2,1)}) custom-call(s32[512]{0:T(512)} %get-tuple-element.15.perm, s32[512]{0:T(512)} %get-tuple-element.14.cols, f32[512]{0:T(512)} %fusion.3.keep, s32[512]{0:T(512)} %add_select_fusion.4.last, bf16[64,4096]{1,0:T(8,128)(2,1)} %feat.3, bf16[512,128,128]{2,1,0:T(8,128)(2,1)} %bitcast.6), custom_call_target="tpu_custom_call" | custom-call | tf_op jit(solution)/shard_map/chain/pallas_call | solution.py:430
  159.1 5.3 %combine.1 = bf16[512,4096]{1,0:T(8,128)(2,1)} custom-call(f32[3,8]{1,0:T(4,128)} %pad_maximum_fusion.coef, bf16[64,4096]{1,0:T(8,128)(2,1)} %feat.3, bf16[2,32,32,128]{3,2,1,0:T(8,128)(2,1)} %get-tuple-element.7.first, bf16[2,32,32,128]{3,2,1,0:T(8,128)(2,1)} %get-tuple-element.8.second), custom_call_target="tpu_custom_call" | custom-call | tf_op jit(solution)/shard_map/combine/pallas_call | solution.py:454

commit v2 on v1

--- a/solution.py
+++ b/solution.py
@@ -10,11 +10,11 @@
 TILE = 128
 SLOTS = 512
 CHANNELS = 64
-CHUNKS = 2
+CHUNKS = 4
 CH = CHANNELS // CHUNKS
 SCALES = 8
 OWN = 32
-UNROLL = 16
+UNROLL = 64
 MESH = pl.DeviceIdType.MESH
 BF = jnp.bfloat16
 F32 = jnp.float32
@@ -63,18 +63,14 @@
 
 def chain_kernel(
     perm, cols, keep, last, feat, tdata, first_out, second_out,
-    tiles, f00, f01, f10, f11, runs, p0, p1,
-    r00, r01, r10, r11, q00, q01, q10, q11,
+    tiles, f00, f01, f02, f03, f10, f11, f12, f13, runs, parts, recv1, recv2,
     tile_sem, s1, v1, s2, v2, sa, va,
 ):
     row = lax.axis_index("row")
     col = lax.axis_index("col")
     z, core = row // 2, row % 2
     y, x = col // 4, col % 4
-    fields = ((f00, f01), (f10, f11))
-    parts = (p0, p1)
-    recv1 = ((r00, r01), (r10, r11))
-    recv2 = ((q00, q01), (q10, q11))
+    fields = ((f00, f01, f02, f03), (f10, f11, f12, f13))
     outs = (first_out, second_out)
 
     def up(v):
@@ -152,7 +148,7 @@
         g[5].start()
         g[10].start()
 
-    def gather_finish(g):
+    def gather_share(g):
         g[1].wait_recv()
         g[8].start()
         g[2].wait_recv()
@@ -161,6 +157,8 @@
         g[11].start()
         g[5].wait_recv()
         g[12].start()
+
+    def gather_finish(g):
         for i in range(6, 13):
             g[i].wait_recv()
 
@@ -170,16 +168,23 @@
 
     def products(a, k, begin, end, acc):
         field = fields[a][k]
+        blank = jnp.zeros((CH, TILE), BF)
 
         def trip(i, acc):
-            for u in range(UNROLL):
+            for u in range(0, UNROLL, 2):
                 s = i * UNROLL + u
-                product = lax.dot_general(
-                    field[cols[s]], tiles[perm[s]], (((1,), (1,)), ((), ())),
-                    preferred_element_type=F32,
+                lhs = jnp.concatenate([
+                    jnp.concatenate([field[cols[s]], blank], axis=1),
+                    jnp.concatenate([blank, field[cols[s + 1]]], axis=1),
+                ], axis=0)
+                rhs = jnp.concatenate([tiles[perm[s]], tiles[perm[s + 1]]], axis=1)
+                pair = lax.dot_general(
+                    lhs, rhs, (((1,), (1,)), ((), ())), preferred_element_type=F32
                 )
-                acc = acc * keep[s] + product
+                acc = acc * keep[s] + pair[:CH]
                 runs[s] = acc.astype(BF)
+                acc = acc * keep[s + 1] + pair[CH:]
+                runs[s + 1] = acc.astype(BF)
             return acc
 
         return lax.fori_loop(begin // UNROLL, end // UNROLL, trip, acc)
@@ -188,7 +193,7 @@
         return jnp.zeros((CH, TILE), F32)
 
     def pack(k):
-        part = parts[k]
+        part = parts.at[k]
 
         def trip(i, carry):
             for xx in range(4):
@@ -200,7 +205,7 @@
         lax.fori_loop(0, 16, trip, 0)
 
     def scatter1(a, k):
-        part, got = parts[k], recv1[a][k]
+        part, got = parts.at[k], recv1.at[a, k]
         out = []
         for st in range(2):
             base = st * 16
@@ -226,7 +231,7 @@
         return out
 
     def scatter2(a, k):
-        part, got = parts[k], recv2[a][k]
+        part, got = parts.at[k], recv2.at[a, k]
         out = []
         for st in range(2):
             base = st * 16
@@ -257,7 +262,7 @@
                 copies[st][d][m].start()
 
     def carry1(a, k, copies):
-        part, got = parts[k], recv1[a][k]
+        part, got = parts.at[k], recv1.at[a, k]
         for st in range(2):
             me = x if st == 0 else y
             for d in range(2):
@@ -280,7 +285,7 @@
                 copies[st][d][2].start()
 
     def close1(a, k, copies):
-        part, got = parts[k], recv1[a][k]
+        part, got = parts.at[k], recv1.at[a, k]
         for m in (1, 2):
             for st in range(2):
                 for d in range(2):
@@ -303,7 +308,7 @@
                 lax.fori_loop(0, 4, trip, 0)
 
     def carry2(a, k, copies):
-        part, got = parts[k], recv2[a][k]
+        part, got = parts.at[k], recv2.at[a, k]
         for st in range(2):
             me = y if st == 0 else x
             for d in range(2):
@@ -319,7 +324,7 @@
                 copies[st][d][2].start()
 
     def close2(a, k, copies):
-        part, got = parts[k], recv2[a][k]
+        part, got = parts.at[k], recv2.at[a, k]
         for m in (1, 2):
             for st in range(2):
                 for d in range(2):
@@ -349,58 +354,58 @@
             fields[0][k][row * OWN + j] = feat[k * CH:(k + 1) * CH, j * TILE:(j + 1) * TILE]
     runs[SLOTS] = jnp.zeros((CH, TILE), BF)
 
+    items = [(a, k) for a in range(2) for k in range(CHUNKS)]
+    total = len(items)
+    g = [gather(a, k) for a, k in items]
+    c1 = [scatter1(a, k) for a, k in items]
+    c2 = [scatter2(a, k) for a, k in items]
+
     pl.semaphore_wait(barrier, 7)
-    g = [[gather(a, k) for k in range(CHUNKS)] for a in range(2)]
-    c1 = [[scatter1(a, k) for k in range(CHUNKS)] for a in range(2)]
-    c2 = [[scatter2(a, k) for k in range(CHUNKS)] for a in range(2)]
-
-    gather_start(g[0][0])
-    gather_relay(g[0][0])
-    gather_start(g[0][1])
-    gather_finish(g[0][0])
-    tile_copy.wait()
-
-    for a in range(2):
-        acc = products(a, 0, 0, SLOTS // 2, zero())
-        gather_relay(g[a][1])
-        products(a, 0, SLOTS // 2, SLOTS, acc)
-        if a == 1:
-            scatter_sent(c1[0][0], c2[0][0])
-        pack(0)
-        start_messages(c1[a][0], 0)
-        start_messages(c1[a][0], 1)
-        gather_finish(g[a][1])
-        products(a, 1, 0, SLOTS, zero())
-        carry1(a, 0, c1[a][0])
-        if a == 1:
-            scatter_sent(c1[0][1], c2[0][1])
-        pack(1)
-        start_messages(c1[a][1], 0)
-        close1(a, 0, c1[a][0])
-        start_messages(c2[a][0], 0)
-        start_messages(c2[a][0], 1)
-        start_messages(c1[a][1], 1)
-        carry2(a, 0, c2[a][0])
-        carry1(a, 1, c1[a][1])
-        close2(a, 0, c2[a][0])
-        if a == 0:
-            gather_start(g[1][0])
-        close1(a, 1, c1[a][1])
-        start_messages(c2[a][1], 0)
-        start_messages(c2[a][1], 1)
-        if a == 0:
-            gather_relay(g[1][0])
-        carry2(a, 1, c2[a][1])
-        if a == 0:
-            gather_finish(g[1][0])
-        close2(a, 1, c2[a][1])
-        if a == 0:
-            gather_start(g[1][1])
-
-    for a in range(2):
-        for k in range(CHUNKS):
-            gather_sent(g[a][k])
-    scatter_sent(c1[1][0], c2[1][0], c1[1][1], c2[1][1])
+    gather_start(g[0])
+    gather_relay(g[0])
+    gather_start(g[1])
+    gather_share(g[0])
+
+    for i in range(-1, total + 2):
+        now, prev, old, nxt = i, i - 1, i - 2, i + 1
+        is_now, is_prev, is_old = 0 <= now < total, 0 <= prev < total, 0 <= old < total
+        is_next = nxt < total
+        if is_prev:
+            close1(*items[prev], c1[prev])
+            start_messages(c2[prev], 0)
+            start_messages(c2[prev], 1)
+        if is_now:
+            start_messages(c1[now], 1)
+        if is_old:
+            close2(*items[old], c2[old])
+            if old < CHUNKS:
+                gather_start(g[old + CHUNKS])
+        if is_next:
+            gather_finish(g[nxt])
+            if nxt == 0:
+                tile_copy.wait()
+            acc = products(*items[nxt], 0, SLOTS // 2, zero())
+        if is_now:
+            carry1(*items[now], c1[now])
+        if is_prev:
+            carry2(*items[prev], c2[prev])
+        if i + 2 < total:
+            gather_relay(g[i + 2])
+        if i + 3 < CHUNKS:
+            gather_start(g[i + 3])
+        if is_next:
+            products(*items[nxt], SLOTS // 2, SLOTS, acc)
+            if nxt >= CHUNKS:
+                scatter_sent(c1[nxt - CHUNKS], c2[nxt - CHUNKS])
+            pack(items[nxt][1])
+            start_messages(c1[nxt], 0)
+        if i + 2 < total:
+            gather_share(g[i + 2])
+
+    for i in range(total):
+        gather_sent(g[i])
+        if i >= CHUNKS:
+            scatter_sent(c1[i], c2[i])
 
 
 def combine_kernel(coef, feat, first, second, out):
@@ -423,9 +428,9 @@
     vmem = pl.BlockSpec(memory_space=pltpu.VMEM)
     half = jax.ShapeDtypeStruct((CHUNKS, OWN, CH, TILE), BF)
     field = pltpu.VMEM((8 * OWN, CH, TILE), BF)
-    part = pltpu.VMEM((4, 4, OWN, CH, TILE), BF)
-    got1 = pltpu.VMEM((2, 2, 3, 4, 8, CH, TILE), BF)
-    got2 = pltpu.VMEM((2, 2, 3, 8, CH, TILE), BF)
+    part = pltpu.VMEM((CHUNKS, 4, 4, OWN, CH, TILE), BF)
+    got1 = pltpu.VMEM((2, CHUNKS, 2, 2, 3, 4, 8, CH, TILE), BF)
+    got2 = pltpu.VMEM((2, CHUNKS, 2, 2, 3, 8, CH, TILE), BF)
     dma = pltpu.SemaphoreType.DMA
     first, second = pl.pallas_call(
         chain_kernel,
@@ -434,11 +439,9 @@
         out_specs=(vmem, vmem),
         scratch_shapes=[
             pltpu.VMEM((SLOTS, TILE, TILE), BF),
-            field, field, field, field,
+            field, field, field, field, field, field, field, field,
             pltpu.VMEM((SLOTS + 1, CH, TILE), BF),
-            part, part,
-            got1, got1, got1, got1,
-            got2, got2, got2, got2,
+            part, got1, got2,
             dma,
             dma((2, CHUNKS, 2, 2, 3)), dma((2, CHUNKS, 2, 2, 3)),
             dma((2, CHUNKS, 2, 2, 3)), dma((2, CHUNKS, 2, 2, 3)),

time: 165 us -> 135 us (0.82)
  Pallas kernels: 159 us -> 129 us
    pallas_call x1, Pallas kernels: 154 us -> 124 us  [shards(): pl.pallas_call(chain_kernel, out_shape=(half, half), in_specs=[smem, smem...]
where the time goes in v2:
time: 135 us; the launch traced here: 134 us
  Pallas kernels  129 us (96%)
  other arithmetic  4.77 us (4%)
    pallas_call x1, Pallas kernels, shards(): pl.pallas_call(chain_kernel, out_shape=(half, half), in_specs=[smem, smem...  124 us
    pallas_call x1, Pallas kernels, shards(): pl.pallas_call(combine_kernel, out_shape=jax.ShapeDtypeStruct((SCALES * C...  5.32 us

profile of v2, /device:TPU:0, one launch (start us, length us, event | category | flops | bytes accessed | tf_op | source)
XLA Modules:
  0.0 134.4 jit_solution(9740469683917563011)
XLA Ops:
  0.7 0.1 broadcast_multiply_fusion
  0.7 0.1 subtract_multiply_fusion
  0.8 0.6 pad_maximum_fusion.coef
  1.4 0.7 iota_add_fusion
  2.1 0.7 multiply_add_fusion
  2.8 0.6 convert_reduce_fusion.1
  3.4 0.2 select_reduce_fusion
  3.6 0.6 add_select_fusion.4.last
  4.2 0.6 add_select_fusion
  4.8 0.6 fusion.3.keep
  5.4 123.6 %chain.1 = (bf16[4,32,16,128]{3,2,1,0:T(8,128)(2,1)}, bf16[4,32,16,128]{3,2,1,0:T(8,128)(2,1)}) custom-call(s32[512]{0:T(512)} %get-tuple-element.15.perm, s32[512]{0:T(512)} %get-tuple-element.14.cols, f32[512]{0:T(512)} %fusion.3.keep, s32[512]{0:T(512)} %add_select_fusion.4.last, bf16[64,4096]{1,0:T(8,128)(2,1)} %feat.3, bf16[512,128,128]{2,1,0:T(8,128)(2,1)} %bitcast.6), custom_call_target="tpu_custom_call" | custom-call | tf_op jit(solution)/shard_map/chain/pallas_call | solution.py:435
  129.1 5.3 %combine.1 = bf16[512,4096]{1,0:T(8,128)(2,1)} custom-call(f32[3,8]{1,0:T(4,128)} %pad_maximum_fusion.coef, bf16[64,4096]{1,0:T(8,128)(2,1)} %feat.3, bf16[4,32,16,128]{3,2,1,0:T(8,128)(2,1)} %get-tuple-element.7.first, bf16[4,32,16,128]{3,2,1,0:T(8,128)(2,1)} %get-tuple-element.8.second), custom_call_target="tpu_custom_call" | custom-call | tf_op jit(solution)/shard_map/combine/pallas_call | solution.py:457

commit v3 on v2

--- a/solution.py
+++ b/solution.py
@@ -2,6 +2,7 @@
 
 import jax
 import jax.numpy as jnp
+import numpy as np
 from jax import lax
 from jax.experimental import pallas as pl
 from jax.experimental.pallas import tpu as pltpu
@@ -15,56 +16,86 @@
 SCALES = 8
 OWN = 32
 UNROLL = 64
+PIECES = 8
 MESH = pl.DeviceIdType.MESH
 BF = jnp.bfloat16
 F32 = jnp.float32
 
 
 def bessel_pair(times):
-    halved = times / 2.0
+    halved = times / np.float32(2.0)
     square = halved * halved
-    term_zero = jnp.ones_like(times)
+    term_zero = np.ones_like(times)
     term_one = halved
     sum_zero = term_zero
     sum_one = term_one
     for degree in range(1, 24):
-        term_zero = term_zero * square / float(degree * degree)
-        term_one = term_one * square / float(degree * (degree + 1))
+        term_zero = term_zero * square / np.float32(degree * degree)
+        term_one = term_one * square / np.float32(degree * (degree + 1))
         sum_zero = sum_zero + term_zero
         sum_one = sum_one + term_one
-    damping = jnp.exp(-times)
+    damping = np.exp(-times)
     return (damping * sum_zero, damping * sum_one)
 
 
 def coefficients():
-    times = 0.25 * 2.0 ** (jnp.arange(SCALES).astype(jnp.float32) / 2.0)
-    bessel_zero, bessel_one = bessel_pair(times)
-    return (bessel_zero, -2.0 * bessel_one, 2.0 * (bessel_zero - 2.0 * bessel_one / times))
-
-
-def slot_tables(slot_rows, slot_cols, live_count):
-    ids = jnp.arange(SLOTS, dtype=jnp.int32)
-    row = jnp.where(ids < live_count, slot_rows, SLOTS)
-    key = row * SLOTS + ids
-    rank = jnp.sum((key[None, :] < key[:, None]).astype(jnp.int32), axis=1)
-    hit = rank[:, None] == ids[None, :]
-    packed = (row * SLOTS + ids) * 256 + slot_cols
-    ordered = jnp.sum(jnp.where(hit, packed[:, None], 0), axis=0)
-    cols = ordered % 256
-    perm = (ordered // 256) % SLOTS
-    rows = ordered // (256 * SLOTS)
-    before = jnp.concatenate([jnp.full((1,), -1, jnp.int32), rows[:-1]])
-    keep = (rows == before).astype(F32)
-    upto = jnp.sum((row[:, None] <= ids[None, :]).astype(jnp.int32), axis=0)
-    here = jnp.sum((row[:, None] == ids[None, :]).astype(jnp.int32), axis=0)
-    last = jnp.where(here > 0, upto - 1, SLOTS)
-    return perm, cols, keep, last
+    two = np.float32(2.0)
+    times = np.float32(0.25) * two ** (np.arange(SCALES).astype(np.float32) / two)
+    bessel_zero, bessel_one = bessel_pair(times.astype(np.float32))
+    return (bessel_zero, -two * bessel_one, two * (bessel_zero - two * bessel_one / times))
+
+
+def flipped(line):
+    return jnp.broadcast_to(line, (TILE, TILE)).T
+
+
+def slot_tables(live, slot_rows, slot_cols, ints, floats):
+    live_count = live[0, 0]
+    lanes = lax.broadcasted_iota(jnp.int32, (1, TILE), 1)
+    deep = lax.broadcasted_iota(jnp.int32, (TILE, TILE), 0).astype(F32)
+    groups = SLOTS // TILE
+    keys, rows_t, keys_t, pairs_t = [], [], [], []
+    for j in range(groups):
+        span = slice(j * TILE, (j + 1) * TILE)
+        ids = lanes + j * TILE
+        rows = jnp.where(ids < live_count, slot_rows[0, :, span], SLOTS).astype(F32)
+        keys.append(rows * SLOTS + ids.astype(F32))
+        rows_t.append(flipped(rows))
+        keys_t.append(flipped(keys[j]))
+        pairs_t.append(rows_t[j] * 256.0 + flipped(slot_cols[0, :, span].astype(F32)))
+
+    def count(masks):
+        total = jnp.zeros((TILE, TILE), F32)
+        for mask in masks:
+            total = total + mask
+        return jnp.sum(total, axis=0, keepdims=True)
+
+    ranks_t = [
+        flipped(count(jnp.where(keys_t[i] < keys[j], 1.0, 0.0) for i in range(groups)))
+        for j in range(groups)
+    ]
+    ints[3 * groups:] = jnp.zeros((4, TILE), jnp.int32)
+    floats[groups:] = jnp.zeros((4, TILE), F32)
+    for j in range(groups):
+        place = (lanes + j * TILE).astype(F32)
+        perm = count(jnp.where(ranks_t[i] == place, deep + float(i * TILE), 0.0) for i in range(groups))
+        pair = count(jnp.where(ranks_t[i] == place, pairs_t[i], 0.0) for i in range(groups))
+        before = count(jnp.where(ranks_t[i] == place - 1.0, rows_t[i], 0.0) for i in range(groups))
+        upto = count(jnp.where(rows_t[i] <= place, 1.0, 0.0) for i in range(groups))
+        here = count(jnp.where(rows_t[i] == place, 1.0, 0.0) for i in range(groups))
+        pair = pair.astype(jnp.int32)
+        rows = pair // 256
+        ints[j:j + 1] = perm.astype(jnp.int32)
+        ints[groups + j:groups + j + 1] = pair - rows * 256
+        ints[2 * groups + j:2 * groups + j + 1] = jnp.where(here > 0.0, upto - 1.0, float(SLOTS)).astype(jnp.int32)
+        floats[j:j + 1] = jnp.where(rows.astype(F32) == before, 1.0, 0.0)
 
 
 def chain_kernel(
-    perm, cols, keep, last, feat, tdata, first_out, second_out,
+    table, keep, feat_hbm, tdata, first_out, second_out,
     tiles, f00, f01, f02, f03, f10, f11, f12, f13, runs, parts, recv1, recv2,
-    tile_sem, s1, v1, s2, v2, sa, va,
+    feat, finals,
+    tile_sem, feat_sem, out_sem, s1, v1, s2, v2, sa, va, sf, vf,
 ):
     row = lax.axis_index("row")
     col = lax.axis_index("col")
@@ -94,8 +125,35 @@
     for other in (z_next, z_prev, mate, x_next, x_prev, y_next, y_prev):
         pl.semaphore_signal(barrier, inc=1, device_id=other, device_id_type=MESH)
 
-    tile_copy = pltpu.make_async_copy(tdata, tiles, tile_sem)
-    tile_copy.start()
+    feat_copies = [
+        pltpu.make_async_copy(
+            feat_hbm.at[pl.ds(k * CH, CH)], feat.at[pl.ds(k * CH, CH)], feat_sem.at[k]
+        )
+        for k in range(CHUNKS)
+    ]
+    for c in feat_copies:
+        c.start()
+
+    piece = SLOTS // PIECES
+    tile_copies = [
+        pltpu.make_async_copy(
+            tdata.at[pl.ds(n * piece, piece)], tiles.at[pl.ds(n * piece, piece)], tile_sem.at[n]
+        )
+        for n in range(PIECES)
+    ]
+    for c in tile_copies:
+        c.start()
+
+    def turn(n):
+        tile_copies[n].wait()
+
+        def trip(i, carry):
+            for u in range(8):
+                t = n * piece + i * 8 + u
+                tiles[t] = tiles[t].T
+            return carry
+
+        lax.fori_loop(0, piece // 8, trip, 0)
 
     def send(src, dst, ssem, rsem, to):
         return pltpu.make_async_remote_copy(
@@ -168,22 +226,21 @@
 
     def products(a, k, begin, end, acc):
         field = fields[a][k]
-        blank = jnp.zeros((CH, TILE), BF)
 
         def trip(i, acc):
+            line, at = i // 2, (i % 2) * UNROLL
             for u in range(0, UNROLL, 2):
                 s = i * UNROLL + u
                 lhs = jnp.concatenate([
-                    jnp.concatenate([field[cols[s]], blank], axis=1),
-                    jnp.concatenate([blank, field[cols[s + 1]]], axis=1),
+                    field[table[4 + line, at + u]], field[table[4 + line, at + u + 1]]
                 ], axis=0)
-                rhs = jnp.concatenate([tiles[perm[s]], tiles[perm[s + 1]]], axis=1)
-                pair = lax.dot_general(
-                    lhs, rhs, (((1,), (1,)), ((), ())), preferred_element_type=F32
-                )
-                acc = acc * keep[s] + pair[:CH]
+                rhs = jnp.concatenate([
+                    tiles[table[line, at + u]], tiles[table[line, at + u + 1]]
+                ], axis=1)
+                pair = jnp.dot(lhs, rhs, preferred_element_type=F32)
+                acc = acc * keep[line, at + u] + pair[:CH, :TILE]
                 runs[s] = acc.astype(BF)
-                acc = acc * keep[s + 1] + pair[CH:]
+                acc = acc * keep[line, at + u + 1] + pair[CH:, TILE:]
                 runs[s + 1] = acc.astype(BF)
             return acc
 
@@ -198,8 +255,7 @@
         def trip(i, carry):
             for xx in range(4):
                 for u in range(8):
-                    b = (i // 4) * 128 + xx * 32 + (i % 4) * 8 + u
-                    part[i // 4, xx, (i % 4) * 8 + u] = runs[last[b]]
+                    part[i // 4, xx, (i % 4) * 8 + u] = runs[table[8 + i // 4, xx * 32 + (i % 4) * 8 + u]]
             return carry
 
         lax.fori_loop(0, 16, trip, 0)
@@ -307,6 +363,77 @@
 
                 lax.fori_loop(0, 4, trip, 0)
 
+    def order(st):
+        me = y if st == 0 else x
+        return (far(me), up(me), down(me), me)
+
+    def scatter1_fine(a, k):
+        part, got = parts.at[k], recv1.at[a, k]
+        out = []
+        for st in range(2):
+            me = x if st == 0 else y
+            rows = []
+            for d in range(2):
+                near = up(me) if d == 0 else down(me)
+                if st == 0:
+                    to = x_next if d == 0 else x_prev
+                else:
+                    to = y_next if d == 0 else y_prev
+                line = []
+                for n, o in enumerate(order(st)):
+                    where = (o, near) if st == 0 else (near, o)
+                    line.append(send(
+                        part.at[where[0], where[1], pl.ds(st * 16 + 8 * d, 8)], got.at[st, d, 2, o],
+                        sf.at[st, d, n], vf.at[st, d, n], to,
+                    ))
+                rows.append(line)
+            out.append(rows)
+        return out
+
+    def carry1_fine(a, k, copies, fine):
+        part, got = parts.at[k], recv1.at[a, k]
+        for st in range(2):
+            for d in range(2):
+                copies[st][d][0].wait_recv()
+        for n in range(4):
+            for st in range(2):
+                me = x if st == 0 else y
+                o = order(st)[n]
+                for d in range(2):
+                    near = up(me) if d == 0 else down(me)
+                    p, q = (o, near) if st == 0 else (near, o)
+                    for u in range(8):
+                        b = st * 16 + 8 * d + u
+                        part[p, q, b] = (
+                            part[p, q, b].astype(F32) + got[st, d, 0, o, u].astype(F32)
+                        ).astype(BF)
+                    fine[st][d][n].start()
+
+    def close1_fine(a, k, copies, fine, later):
+        part, got = parts.at[k], recv1.at[a, k]
+        for st in range(2):
+            for d in range(2):
+                copies[st][d][1].wait_recv()
+        for n in range(4):
+            for st in range(2):
+                o = order(st)[n]
+                for d in range(2):
+                    fine[st][d][n].wait_recv()
+                p, q = (o, x) if st == 0 else (y, o)
+                for h in range(2):
+                    for u in range(8):
+                        b = st * 16 + 8 * h + u
+                        part[p, q, b] = (
+                            part[p, q, b].astype(F32)
+                            + got[st, h, 2, o, u].astype(F32)
+                            + got[st, 1 - h, 1, o, u].astype(F32)
+                        ).astype(BF)
+                if n == 0:
+                    later[st][0][0].start()
+                    later[st][1][0].start()
+                elif n < 3:
+                    later[st][n - 1][1].start()
+
     def carry2(a, k, copies):
         part, got = parts.at[k], recv2.at[a, k]
         for st in range(2):
@@ -338,9 +465,14 @@
                         + got[st, h, 2, u].astype(F32)
                         + got[st, 1 - h, 1, u].astype(F32)
                     ).astype(BF)
-                    outs[a][k, b] = total
                     if a == 0:
                         fields[1][k][row * OWN + b] = total
+                    else:
+                        finals[k, b] = total
+
+    def deliver(a, k):
+        source = fields[1][k].at[pl.ds(row * OWN, OWN)] if a == 0 else finals.at[k]
+        return pltpu.make_async_copy(source, outs[a].at[k], out_sem.at[a, k])
 
     def scatter_sent(*many):
         for copies in many:
@@ -349,24 +481,36 @@
                     for m in range(3):
                         copies[st][d][m].wait_send()
 
-    for k in range(CHUNKS):
+    def own(k):
+        feat_copies[k].wait()
         for j in range(OWN):
             fields[0][k][row * OWN + j] = feat[k * CH:(k + 1) * CH, j * TILE:(j + 1) * TILE]
-    runs[SLOTS] = jnp.zeros((CH, TILE), BF)
 
     items = [(a, k) for a in range(2) for k in range(CHUNKS)]
     total = len(items)
     g = [gather(a, k) for a, k in items]
     c1 = [scatter1(a, k) for a, k in items]
     c2 = [scatter2(a, k) for a, k in items]
-
+    deliveries = [deliver(a, k) for a, k in items]
+    fine = scatter1_fine(*items[-1])
+
+    own(0)
     pl.semaphore_wait(barrier, 7)
     gather_start(g[0])
+    for k in range(1, CHUNKS):
+        own(k)
+    runs[SLOTS] = jnp.zeros((CH, TILE), BF)
+    turn(0)
+    turn(1)
     gather_relay(g[0])
     gather_start(g[1])
+    for n in range(2, 5):
+        turn(n)
     gather_share(g[0])
-
-    for i in range(-1, total + 2):
+    for n in range(5, PIECES):
+        turn(n)
+
+    for i in range(-1, total):
         now, prev, old, nxt = i, i - 1, i - 2, i + 1
         is_now, is_prev, is_old = 0 <= now < total, 0 <= prev < total, 0 <= old < total
         is_next = nxt < total
@@ -378,17 +522,20 @@
             start_messages(c1[now], 1)
         if is_old:
             close2(*items[old], c2[old])
+            deliveries[old].start()
             if old < CHUNKS:
                 gather_start(g[old + CHUNKS])
         if is_next:
             gather_finish(g[nxt])
-            if nxt == 0:
-                tile_copy.wait()
             acc = products(*items[nxt], 0, SLOTS // 2, zero())
-        if is_now:
-            carry1(*items[now], c1[now])
-        if is_prev:
+        if now == total - 1:
             carry2(*items[prev], c2[prev])
+            carry1_fine(*items[now], c1[now], fine)
+        else:
+            if is_now:
+                carry1(*items[now], c1[now])
+            if is_prev:
+                carry2(*items[prev], c2[prev])
         if i + 2 < total:
             gather_relay(g[i + 2])
         if i + 3 < CHUNKS:
@@ -402,65 +549,102 @@
         if i + 2 < total:
             gather_share(g[i + 2])
 
+    close1_fine(*items[-1], c1[-1], fine, c2[-1])
+    carry2(*items[-1], c2[-1])
+    close2(*items[-2], c2[-2])
+    deliveries[-2].start()
+    close2(*items[-1], c2[-1])
+    deliveries[-1].start()
+
     for i in range(total):
         gather_sent(g[i])
-        if i >= CHUNKS:
+        if i == total - 1:
+            for st in range(2):
+                for d in range(2):
+                    for m in range(2):
+                        c1[i][st][d][m].wait_send()
+                    for c in fine[st][d]:
+                        c.wait_send()
+            scatter_sent(c2[i])
+        elif i >= CHUNKS:
             scatter_sent(c1[i], c2[i])
-
-
-def combine_kernel(coef, feat, first, second, out):
+        deliveries[i].wait()
+
+
+def combine_kernel(coef, feat, first, second, out, stage, sem):
+    copies = []
     for k in range(CHUNKS):
+        channels = slice(k * CH, (k + 1) * CH)
         for j in range(OWN):
             nodes = slice(j * TILE, (j + 1) * TILE)
-            base = feat[k * CH:(k + 1) * CH, nodes].astype(F32)
+            base = feat[channels, nodes].astype(F32)
             one = first[k, j].astype(F32)
             two = 2.0 * second[k, j].astype(F32) - base
             for s in range(SCALES):
-                value = coef[0, s] * base + coef[1, s] * one + coef[2, s] * two
-                out[s * CHANNELS + k * CH:s * CHANNELS + (k + 1) * CH, nodes] = value.astype(BF)
+                value = coef[0][s] * base + coef[1][s] * one + coef[2][s] * two
+                stage[s * CHANNELS + k * CH:s * CHANNELS + (k + 1) * CH, nodes] = value.astype(BF)
+        for s in range(SCALES):
+            block = pl.ds(s * CHANNELS + k * CH, CH)
+            copies.append(pltpu.make_async_copy(stage.at[block], out.at[block], sem.at[k, s]))
+            copies[-1].start()
+    for c in copies:
+        c.wait()
 
 
 def shards(features, tile_rows, tile_cols, tile_count, tile_data):
-    perm, cols, keep, last = slot_tables(
-        tile_rows.reshape(-1), tile_cols.reshape(-1), tile_count.reshape(())
-    )
     smem = pl.BlockSpec(memory_space=pltpu.SMEM)
     vmem = pl.BlockSpec(memory_space=pltpu.VMEM)
+    hbm = pl.BlockSpec(memory_space=pl.ANY)
     half = jax.ShapeDtypeStruct((CHUNKS, OWN, CH, TILE), BF)
     field = pltpu.VMEM((8 * OWN, CH, TILE), BF)
     part = pltpu.VMEM((CHUNKS, 4, 4, OWN, CH, TILE), BF)
     got1 = pltpu.VMEM((2, CHUNKS, 2, 2, 3, 4, 8, CH, TILE), BF)
     got2 = pltpu.VMEM((2, CHUNKS, 2, 2, 3, 8, CH, TILE), BF)
     dma = pltpu.SemaphoreType.DMA
+    table, keep = pl.pallas_call(
+        slot_tables,
+        out_shape=(
+            jax.ShapeDtypeStruct((16, TILE), jnp.int32), jax.ShapeDtypeStruct((8, TILE), F32)
+        ),
+        in_specs=[smem, vmem, vmem],
+        out_specs=(vmem, vmem),
+        name="tables",
+    )(tile_count, tile_rows, tile_cols)
     first, second = pl.pallas_call(
         chain_kernel,
         out_shape=(half, half),
-        in_specs=[smem, smem, smem, smem, vmem, pl.BlockSpec(memory_space=pl.ANY)],
-        out_specs=(vmem, vmem),
+        in_specs=[smem, smem, hbm, hbm],
+        out_specs=(hbm, hbm),
         scratch_shapes=[
             pltpu.VMEM((SLOTS, TILE, TILE), BF),
             field, field, field, field, field, field, field, field,
             pltpu.VMEM((SLOTS + 1, CH, TILE), BF),
             part, got1, got2,
-            dma,
+            pltpu.VMEM((CHANNELS, OWN * TILE), BF), pltpu.VMEM((CHUNKS, OWN, CH, TILE), BF),
+            dma((PIECES,)), dma((CHUNKS,)), dma((2, CHUNKS)),
             dma((2, CHUNKS, 2, 2, 3)), dma((2, CHUNKS, 2, 2, 3)),
             dma((2, CHUNKS, 2, 2, 3)), dma((2, CHUNKS, 2, 2, 3)),
             dma((2, CHUNKS, 13)), dma((2, CHUNKS, 13)),
+            dma((2, 2, 4)), dma((2, 2, 4)),
         ],
         compiler_params=pltpu.CompilerParams(
             collective_id=0, has_side_effects=True, vmem_limit_bytes=62 * 1024 * 1024
         ),
         name="chain",
-    )(perm, cols, keep, last, features, tile_data.reshape(SLOTS, TILE, TILE))
-
-    coef = jnp.stack(coefficients())
+    )(table, keep, features, tile_data.reshape(SLOTS, TILE, TILE))
+
+    coef = [[float(value) for value in line] for line in coefficients()]
     return pl.pallas_call(
-        combine_kernel,
+        functools.partial(combine_kernel, coef),
         out_shape=jax.ShapeDtypeStruct((SCALES * CHANNELS, OWN * TILE), BF),
-        in_specs=[smem, vmem, vmem, vmem],
-        out_specs=vmem,
+        in_specs=[vmem, vmem, vmem],
+        out_specs=hbm,
+        scratch_shapes=[
+            pltpu.VMEM((SCALES * CHANNELS, OWN * TILE), BF),
+            dma((CHUNKS, SCALES)),
+        ],
         name="combine",
-    )(coef, features, first, second)
+    )(features, first, second)
 
 
 def solution(mesh):

time: 135 us -> 130 us (0.963)
  other arithmetic: 4.77 us -> 0 us
    pallas_call x1, Pallas kernels: 124 us -> 122 us  [shards(): pl.pallas_call(chain_kernel, out_shape=(half, half), in_specs=[smem, smem...]
    add x2 -> x0, other arithmetic: 1.37 us -> none  [the longest x1 0.69 us: slot_tables(): key = row * SLOTS + ids]
    pallas_call x1 -> x2, Pallas kernels: 5.32 us -> 6.57 us  [the longest x1 4.45 us: shards(): pl.pallas_call(functools.partial(combine_kernel, coef), out_shape=jax.Sha...]
where the time goes in v3:
time: 130 us; the launch traced here: 129 us
  Pallas kernels  129 us (99%)
    pallas_call x1, Pallas kernels, shards(): pl.pallas_call(chain_kernel, out_shape=(half, half), in_specs=[smem, smem...  122 us
    pallas_call x1, Pallas kernels, shards(): pl.pallas_call(functools.partial(combine_kernel, coef), out_shape=jax.Sha...  4.45 us

profile of v3, /device:TPU:0, one launch (start us, length us, event | category | flops | bytes accessed | tf_op | source)
XLA Modules:
  0.0 129.5 jit_solution(12748223822588925656)
XLA Ops:
  0.7 2.1 %tables.1 = (s32[16,128]{1,0:T(8,128)}, f32[8,128]{1,0:T(8,128)}) custom-call(s32[1,1]{1,0:T(1,128)S(6)} %copy.6.live, s32[1,1,512]{2,1,0:T(1,128)} %slot_rows.1, s32[1,1,512]{2,1,0:T(1,128)} %slot_cols.1), custom_call_target="tpu_custom_call" | custom-call | tf_op jit(solution)/shard_map/tables/pallas_call | solution.py:604
  2.8 122.1 %chain.1 = (bf16[4,32,16,128]{3,2,1,0:T(8,128)(2,1)}, bf16[4,32,16,128]{3,2,1,0:T(8,128)(2,1)}) custom-call(s32[16,128]{1,0:T(8,128)} %get-tuple-element.9.table, f32[8,128]{1,0:T(8,128)} %get-tuple-element.10.keep, bf16[64,4096]{1,0:T(8,128)(2,1)} %feat.1, bf16[512,128,128]{2,1,0:T(8,128)(2,1)} %bitcast.1), custom_call_target="tpu_custom_call" | custom-call | tf_op jit(solution)/shard_map/chain/pallas_call | solution.py:613
  124.8 4.5 %combine.1 = bf16[512,4096]{1,0:T(8,128)(2,1)} custom-call(bf16[64,4096]{1,0:T(8,128)(2,1)} %feat.1, bf16[4,32,16,128]{3,2,1,0:T(8,128)(2,1)} %get-tuple-element.11.first, bf16[4,32,16,128]{3,2,1,0:T(8,128)(2,1)} %get-tuple-element.12.second), custom_call_target="tpu_custom_call" | custom-call | tf_op jit(solution)/shard_map/combine/pallas_call | solution.py:637
